TPU v7x, 32 devices: a whole 2x2x4 slice. The times are simulated.
32 devices in a mesh: left: 8 (over z, x), right: 4 (over y, core).
Axes of the slice: x: 2, y: 2, z: 4, core: 2. Of those that a mesh axis runs over, the one named last changes fastest.
Arguments:
- species: float32 [4, 256, 128, 128], P(None, None, 'left', 'right'), may hold values from -6 to 6
- coupling: float32 [4, 4], replicated, may hold values from -4 to 4
- symbol_x: float32 [256], replicated, may hold values from 0.3 to 3
- symbol_y: float32 [128], replicated, may hold values from 0.3 to 3
- symbol_z: float32 [128], replicated, may hold values from 0.3 to 3
Outputs:
- modes: float32 [4, 256, 128, 128], P(None, 'left', 'right')
All inputs are finite; a program needn't handle non-finite values.
Results may differ from a plain program's by a relative error of at most 0.000071.
Values sent between devices are 32-bit elements; how exact they have to be, the bound alone decides.
A program may use at most 128 MiB of HBM per device.

v0:
```python
import functools

import jax
import jax.numpy as jnp
import numpy as np
from jax import lax
from jax.experimental import pallas as pl
from jax.experimental.pallas import tpu as pltpu
from jax.sharding import PartitionSpec as P

MESH = pl.DeviceIdType.MESH
AHEAD = 2


def chunk_sizes(block):
    unit = block // 16
    return [part * unit for part in (3, 3, 3, 3, 2, 2)] if unit % 2 == 0 and unit else [block]


def basis_table(count):
    rank = np.arange(count)
    angle = 2.0 * np.pi / count * (rank[:, None] * rank[None, :] % count)
    return (np.cos(angle) + np.sin(angle)) / np.sqrt(count)


def halves(table):
    table = table.astype(np.float32)
    high = table.astype(jnp.bfloat16)
    low = (table - high.astype(np.float32)).astype(jnp.bfloat16)
    return high, low


def split(values):
    high = values.astype(jnp.bfloat16)
    low = (values - high.astype(jnp.float32)).astype(jnp.bfloat16)
    return high, low


def kernel(
    n_left, n_right, sizes,
    x_hbm, hx_hbm, hy_hbm, wz_hbm, coup_hbm, sx_hbm, sy_hbm, sz_hbm,
    out_ref,
    x_buf, hx, hy, wz, coup_ref, sx_ref, sy_ref, sz_ref, send_a, recv_b, send_c, recv_d, z_buf, sy_cols,
    sem_x, sem_t, sem_as, sem_br, sem_cs, sem_dr,
):
    fields, share_y, share_z, size_x = x_hbm.shape
    size_y, size_z = sy_hbm.shape[1], sz_hbm.shape[1]
    lanes = fields * share_z
    block_x, block_y = size_x // n_left, size_y // n_right
    pairs = share_y // 2
    starts = [sum(sizes[:c]) for c in range(len(sizes))]
    left, right = lax.axis_index("left"), lax.axis_index("right")
    hops_left = sorted(range(1, n_left), key=lambda j: (abs(2 * j - n_left), j))
    hops_right = sorted(range(1, n_right), key=lambda j: (abs(2 * j - n_right), j))

    table_copies = [
        pltpu.make_async_copy(src, dst, sem_t.at[i])
        for i, (src, dst) in enumerate((
            (hx_hbm, hx), (hy_hbm, hy), (wz_hbm, wz), (coup_hbm, coup_ref),
            (sx_hbm, sx_ref), (sy_hbm, sy_ref), (sz_hbm, sz_ref),
        ))
    ]

    def x_copy(pair):
        return pltpu.make_async_copy(
            x_hbm.at[:, pl.ds(2 * pair, 2)], x_buf.at[pair], sem_x.at[pair]
        )

    barrier = pltpu.get_barrier_semaphore()
    for j in hops_left:
        pl.semaphore_signal(
            barrier, inc=1, device_id=(lax.rem(left + j, n_left), right), device_id_type=MESH
        )
    for j in hops_right:
        pl.semaphore_signal(
            barrier, inc=1, device_id=(left, lax.rem(right + j, n_right)), device_id_type=MESH
        )
    table_copies[0].start()
    for pair in range(pairs):
        x_copy(pair).start()
    for copy in table_copies[1:]:
        copy.start()

    def left_copy(chunk, j):
        other = lax.rem(left + j, n_left)
        start, size = starts[chunk], sizes[chunk]
        return pltpu.make_async_remote_copy(
            src_ref=send_a.at[pl.ds(start * n_left + other * size, size)],
            dst_ref=recv_b.at[pl.ds(start, size), pl.ds(left * share_y, share_y)],
            send_sem=sem_as.at[chunk, j],
            recv_sem=sem_br.at[chunk, j],
            device_id=(other, right),
            device_id_type=MESH,
        )

    def right_copy(chunk, j):
        other = lax.rem(right + j, n_right)
        rows = pl.ds(starts[chunk], sizes[chunk])
        return pltpu.make_async_remote_copy(
            src_ref=send_c.at[other, rows],
            dst_ref=recv_d.at[right, rows],
            send_sem=sem_cs.at[chunk, j],
            recv_sem=sem_dr.at[chunk, j],
            device_id=(left, other),
            device_id_type=MESH,
        )

    flat_a = send_a.reshape(size_x * share_y, lanes)

    def x_step(pair, carry):
        x_copy(pair).wait()
        planes = [x_buf[pair, :, i].reshape(lanes, size_x) for i in range(2)]
        high, low = split(jnp.concatenate(planes, axis=0))
        dot = functools.partial(
            lax.dot_general,
            dimension_numbers=(((1,), (1,)), ((), ())),
            preferred_element_type=jnp.float32,
        )
        both = dot(hx[...], high)
        modes = both[:size_x] + both[size_x:] + dot(hx[:size_x], low)
        for i in range(2):
            flat_a[pl.ds(2 * pair + i, size_x, stride=share_y), :] = modes[
                :, i * lanes:(i + 1) * lanes
            ]
        return carry

    table_copies[0].wait()
    lax.fori_loop(0, pairs, x_step, 0)
    pl.semaphore_wait(barrier, n_left + n_right - 2)
    def left_start(chunk):
        if chunk < len(sizes):
            for j in hops_left:
                left_copy(chunk, j).start()

    for chunk in range(AHEAD):
        left_start(chunk)

    for start, size in zip(starts, sizes):
        recv_b[pl.ds(start, size), pl.ds(left * share_y, share_y)] = send_a[
            pl.ds(start * n_left + left * size, size)
        ]
    for copy in table_copies[1:]:
        copy.wait()
    sy_cols[...] = jnp.broadcast_to(sy_ref[...], (size_z, size_y)).T

    def y_stage(chunk):
        for j in hops_left:
            left_copy(chunk, j).wait_recv()
        left_start(chunk + AHEAD)
        start, size = starts[chunk], sizes[chunk]

        def y_step(step, carry):
            rows = [recv_b[start + 2 * step + i] for i in range(2)]
            high, low = split(jnp.concatenate(rows, axis=1))
            dot = functools.partial(jnp.dot, preferred_element_type=jnp.float32)
            both = dot(hy[...], high)
            modes = both[:size_y] + both[size_y:] + dot(hy[:size_y], low)
            for i in range(2):
                send_c[:, start + 2 * step + i] = modes[:, i * lanes:(i + 1) * lanes].reshape(
                    n_right, block_y, lanes
                )
            return carry

        lax.fori_loop(0, size // 2, y_step, 0)
        for j in hops_right:
            right_copy(chunk, j).start()
        recv_d[right, pl.ds(start, size)] = send_c[right, pl.ds(start, size)]

    def z_stage(chunk):
        for j in hops_right:
            right_copy(chunk, j).wait_recv()
        start, size = starts[chunk], sizes[chunk]
        count = size * block_y
        lines = [
            recv_d[r, pl.ds(start, size)].reshape(count, lanes) for r in range(n_right)
        ]
        high, low = split(jnp.concatenate(lines, axis=1))
        dot = functools.partial(jnp.dot, preferred_element_type=jnp.float32)
        z_buf[:count] = dot(high, wz[0]) + dot(low, wz[0]) + dot(high, wz[1])

        part_y = sy_cols[pl.ds(pl.multiple_of(right * block_y, block_y), block_y), :]

        def mix_step(step, carry):
            symbol = sx_ref[0, left * block_x + start + step] + part_y + sz_ref[...]
            weight = 1.0 / (1.0 + symbol)
            rest = 1.0 - weight
            rows = pl.ds(pl.multiple_of(step * block_y, block_y), block_y)
            old = [z_buf[rows, b * size_z:(b + 1) * size_z] for b in range(fields)]
            for a in range(fields):
                mixed = coup_ref[a, 0] * old[0]
                for b in range(1, fields):
                    mixed += coup_ref[a, b] * old[b]
                out_ref[a, start + step] = weight * old[a] + rest * mixed
            return carry

        lax.fori_loop(0, size, mix_step, 0)

    for chunk in range(len(sizes)):
        y_stage(chunk)
        if chunk:
            z_stage(chunk - 1)
    z_stage(len(sizes) - 1)

    for chunk in range(len(sizes)):
        for j in hops_left:
            left_copy(chunk, j).wait_send()
        for j in hops_right:
            right_copy(chunk, j).wait_send()


def solution(mesh):
    n_left, n_right = mesh.shape["left"], mesh.shape["right"]

    def body(species, coupling, symbol_x, symbol_y, symbol_z):
        fields, size_x, share_y, share_z = species.shape
        size_y, size_z = symbol_y.shape[0], symbol_z.shape[0]
        lanes = fields * share_z
        block_x, block_y = size_x // n_left, size_y // n_right
        sizes = chunk_sizes(block_x)
        chunks = len(sizes)

        order = np.concatenate([
            np.arange(size_x).reshape(n_left, block_x)[:, sum(sizes[:c]):sum(sizes[:c + 1])].ravel()
            for c in range(chunks)
        ])
        hx = np.concatenate(halves(basis_table(size_x)[order]))
        hy = np.concatenate(halves(basis_table(size_y)))
        hz = basis_table(size_z).reshape(n_right, share_z, size_z)
        wz = np.einsum("rzn,fg->rfzgn", hz, np.eye(fields))
        wz = np.stack(halves(wz.reshape(n_right * lanes, fields * size_z)))

        hbm = pl.BlockSpec(memory_space=pltpu.HBM)
        vmem = pl.BlockSpec(memory_space=pltpu.VMEM)
        f32, bf16 = jnp.float32, jnp.bfloat16
        room = 64 * 2 ** 20 - 2 * (4 * fields * block_x * block_y * size_z)
        return pl.pallas_call(
            functools.partial(kernel, n_left, n_right, sizes),
            out_shape=pltpu.VMEM((fields, block_x, block_y, size_z), f32),
            in_specs=[hbm] * 8,
            out_specs=vmem,
            scratch_shapes=[
                pltpu.VMEM((share_y // 2, fields, 2, share_z, size_x), f32),
                pltpu.VMEM(hx.shape, bf16),
                pltpu.VMEM(hy.shape, bf16),
                pltpu.VMEM(wz.shape, bf16),
                pltpu.SMEM(coupling.shape, f32),
                pltpu.SMEM((1, size_x), f32),
                pltpu.VMEM((1, size_y), f32),
                pltpu.VMEM((1, size_z), f32),
                pltpu.VMEM((size_x, share_y, lanes), f32),
                pltpu.VMEM((block_x, size_y, lanes), f32),
                pltpu.VMEM((n_right, block_x, block_y, lanes), f32),
                pltpu.VMEM((n_right, block_x, block_y, lanes), f32),
                pltpu.VMEM((max(sizes) * block_y, fields * size_z), f32),
                pltpu.VMEM((size_y, size_z), f32),
                pltpu.SemaphoreType.DMA((share_y // 2,)),
                pltpu.SemaphoreType.DMA((7,)),
                pltpu.SemaphoreType.DMA((chunks, n_left)),
                pltpu.SemaphoreType.DMA((chunks, n_left)),
                pltpu.SemaphoreType.DMA((chunks, n_right)),
                pltpu.SemaphoreType.DMA((chunks, n_right)),
            ],
            compiler_params=pltpu.CompilerParams(
                collective_id=0, has_side_effects=True, vmem_limit_bytes=room
            ),
        )(
            jnp.transpose(species, (0, 2, 3, 1)), jnp.asarray(hx), jnp.asarray(hy),
            jnp.asarray(wz), coupling, symbol_x[None], symbol_y[None], symbol_z[None],
        )

    in_specs = (P(None, None, "left", "right"), P(), P(), P(), P())
    out_specs = P(None, "left", "right", None)
    return jax.shard_map(body, mesh=mesh, in_specs=in_specs, out_specs=out_specs, check_vma=False)
```

profile of v0, /device:TPU:0, one launch (start us, length us, event | category | flops | bytes accessed | tf_op | source)
XLA Modules:
  0.0 61.5 jit_solution(6695810257106867407)
XLA Ops:
  0.0 60.2 %shard_map.82 = f32[4,32,32,128]{3,2,1,0:T(8,128)S(1)} custom-call(f32[4,16,32,256]{3,2,1,0:T(8,128)} %bitcast.4, bf16[512,256]{1,0:T(8,128)(2,1)} %constant.6.clone.hx_hbm, bf16[256,128]{1,0:T(8,128)(2,1)} %constant.7.clone.hy_hbm, bf16[2,512,512]{2,1,0:T(8,128)(2,1)} %constant.8.clone.wz_hbm, f32[4,4]{1,0:T(4,128)} %coup_hbm.1, f32[1,256]{1,0:T(1,128)} %bitcast.5, ...), custom_call_target="tpu_custom_call" | custom-call | tf_op jit(solution)/shard_map/pallas_call | solution.py:236
  60.2 1.3 %copy.10 = f32[4,32,32,128]{3,2,1,0:T(8,128)} copy(f32[4,32,32,128]{3,2,1,0:T(8,128)S(1)} %shard_map.82) | data formatting | bytes 4194304
where the time goes:
time: 61.7 us; the launch traced here: 61.5 us
  Pallas kernels  60.2 us (98%)
  local copies, waits for them, and re-layouts  1.32 us (2%)
    pallas_call x1, Pallas kernels, body(): pl.pallas_call(functools.partial(kernel, n_left, n_right, sizes), out_sha...  60.2 us
    unnamed x1, local copies, waits for them, and re-layouts  1.32 us

commit v1 on v0

--- a/solution.py
+++ b/solution.py
@@ -9,12 +9,14 @@
 from jax.sharding import PartitionSpec as P
 
 MESH = pl.DeviceIdType.MESH
-AHEAD = 2
+WINDOW = 12
+PARTS = (6, 6, 6, 6, 4, 4)
+GROUPS = 4
 
 
 def chunk_sizes(block):
-    unit = block // 16
-    return [part * unit for part in (3, 3, 3, 3, 2, 2)] if unit % 2 == 0 and unit else [block]
+    unit = block // sum(PARTS)
+    return [part * unit for part in PARTS] if unit and block % sum(PARTS) == 0 else [block]
 
 
 def basis_table(count):
@@ -50,6 +52,9 @@
     pairs = share_y // 2
     starts = [sum(sizes[:c]) for c in range(len(sizes))]
     left, right = lax.axis_index("left"), lax.axis_index("right")
+    ends = [start + size for start, size in zip(starts, sizes)]
+    groups = GROUPS if pairs % GROUPS == 0 else 1
+    group_y = share_y // groups
     hops_left = sorted(range(1, n_left), key=lambda j: (abs(2 * j - n_left), j))
     hops_right = sorted(range(1, n_right), key=lambda j: (abs(2 * j - n_right), j))
 
@@ -81,14 +86,18 @@
     for copy in table_copies[1:]:
         copy.start()
 
-    def left_copy(chunk, j):
+    def left_copy(chunk, j, first_y=0, count_y=share_y):
         other = lax.rem(left + j, n_left)
         start, size = starts[chunk], sizes[chunk]
         return pltpu.make_async_remote_copy(
-            src_ref=send_a.at[pl.ds(start * n_left + other * size, size)],
-            dst_ref=recv_b.at[pl.ds(start, size), pl.ds(left * share_y, share_y)],
-            send_sem=sem_as.at[chunk, j],
-            recv_sem=sem_br.at[chunk, j],
+            src_ref=send_a.at[
+                pl.ds(start * n_left + other * size, size), pl.ds(first_y, count_y)
+            ],
+            dst_ref=recv_b.at[
+                pl.ds(start, size), pl.ds(left * share_y + first_y, count_y)
+            ],
+            send_sem=sem_as.at[0],
+            recv_sem=sem_br.at[chunk],
             device_id=(other, right),
             device_id_type=MESH,
         )
@@ -99,11 +108,22 @@
         return pltpu.make_async_remote_copy(
             src_ref=send_c.at[other, rows],
             dst_ref=recv_d.at[right, rows],
-            send_sem=sem_cs.at[chunk, j],
-            recv_sem=sem_dr.at[chunk, j],
+            send_sem=sem_cs.at[0],
+            recv_sem=sem_dr.at[chunk],
             device_id=(left, other),
             device_id_type=MESH,
         )
+
+    def wait_bytes(ref, sem):
+        pltpu.make_async_copy(ref, ref, sem).wait()
+
+    def left_arrived(chunk):
+        rows = pl.ds(starts[chunk], sizes[chunk])
+        wait_bytes(recv_b.at[rows, pl.ds(0, (n_left - 1) * share_y)], sem_br.at[chunk])
+
+    def right_arrived(chunk):
+        rows = pl.ds(starts[chunk], sizes[chunk])
+        wait_bytes(recv_d.at[pl.ds(0, n_right - 1), rows], sem_dr.at[chunk])
 
     flat_a = send_a.reshape(size_x * share_y, lanes)
 
@@ -125,15 +145,21 @@
         return carry
 
     table_copies[0].wait()
-    lax.fori_loop(0, pairs, x_step, 0)
-    pl.semaphore_wait(barrier, n_left + n_right - 2)
-    def left_start(chunk):
-        if chunk < len(sizes):
-            for j in hops_left:
-                left_copy(chunk, j).start()
-
-    for chunk in range(AHEAD):
-        left_start(chunk)
+    per_group = pairs // groups
+    for group in range(groups):
+        lax.fori_loop(group * per_group, (group + 1) * per_group, x_step, 0)
+        if group == 0:
+            pl.semaphore_wait(barrier, n_left + n_right - 2)
+        for j in hops_left:
+            left_copy(0, j, group * group_y, group_y).start()
+
+    def left_start(after, upto):
+        for chunk in range(1, len(sizes)):
+            if after < ends[chunk] <= upto:
+                for j in hops_left:
+                    left_copy(chunk, j).start()
+
+    left_start(ends[0], max(WINDOW, ends[0]))
 
     for start, size in zip(starts, sizes):
         recv_b[pl.ds(start, size), pl.ds(left * share_y, share_y)] = send_a[
@@ -144,9 +170,8 @@
     sy_cols[...] = jnp.broadcast_to(sy_ref[...], (size_z, size_y)).T
 
     def y_stage(chunk):
-        for j in hops_left:
-            left_copy(chunk, j).wait_recv()
-        left_start(chunk + AHEAD)
+        left_arrived(chunk)
+        left_start(max(starts[chunk] + WINDOW, ends[0]), ends[chunk] + WINDOW)
         start, size = starts[chunk], sizes[chunk]
 
         def y_step(step, carry):
@@ -167,8 +192,7 @@
         recv_d[right, pl.ds(start, size)] = send_c[right, pl.ds(start, size)]
 
     def z_stage(chunk):
-        for j in hops_right:
-            right_copy(chunk, j).wait_recv()
+        right_arrived(chunk)
         start, size = starts[chunk], sizes[chunk]
         count = size * block_y
         lines = [
@@ -201,11 +225,8 @@
             z_stage(chunk - 1)
     z_stage(len(sizes) - 1)
 
-    for chunk in range(len(sizes)):
-        for j in hops_left:
-            left_copy(chunk, j).wait_send()
-        for j in hops_right:
-            right_copy(chunk, j).wait_send()
+    wait_bytes(send_a.at[pl.ds(0, (n_left - 1) * block_x)], sem_as.at[0])
+    wait_bytes(send_c.at[pl.ds(0, n_right - 1)], sem_cs.at[0])
 
 
 def solution(mesh):
@@ -255,10 +276,10 @@
                 pltpu.VMEM((size_y, size_z), f32),
                 pltpu.SemaphoreType.DMA((share_y // 2,)),
                 pltpu.SemaphoreType.DMA((7,)),
-                pltpu.SemaphoreType.DMA((chunks, n_left)),
-                pltpu.SemaphoreType.DMA((chunks, n_left)),
-                pltpu.SemaphoreType.DMA((chunks, n_right)),
-                pltpu.SemaphoreType.DMA((chunks, n_right)),
+                pltpu.SemaphoreType.DMA((1,)),
+                pltpu.SemaphoreType.DMA((chunks,)),
+                pltpu.SemaphoreType.DMA((1,)),
+                pltpu.SemaphoreType.DMA((chunks,)),
             ],
             compiler_params=pltpu.CompilerParams(
                 collective_id=0, has_side_effects=True, vmem_limit_bytes=room

time: 61.7 us -> 58.9 us (0.955)
  Pallas kernels: 60.2 us -> 57.4 us
    pallas_call x1, Pallas kernels: 60.2 us -> 57.4 us  [body(): pl.pallas_call(functools.partial(kernel, n_left, n_right, sizes), out_sha...]
where the time goes in v1:
time: 58.9 us; the launch traced here: 58.7 us
  Pallas kernels  57.4 us (97%)
  local copies, waits for them, and re-layouts  1.32 us (2%)
    pallas_call x1, Pallas kernels, body(): pl.pallas_call(functools.partial(kernel, n_left, n_right, sizes), out_sha...  57.4 us
    unnamed x1, local copies, waits for them, and re-layouts  1.32 us

profile of v1, /device:TPU:0, one launch (start us, length us, event | category | flops | bytes accessed | tf_op | source)
XLA Modules:
  0.0 58.7 jit_solution(2309843006967927223)
XLA Ops:
  0.0 57.4 %shard_map.82 = f32[4,32,32,128]{3,2,1,0:T(8,128)S(1)} custom-call(f32[4,16,32,256]{3,2,1,0:T(8,128)} %bitcast.4, bf16[512,256]{1,0:T(8,128)(2,1)} %constant.6.clone.hx_hbm, bf16[256,128]{1,0:T(8,128)(2,1)} %constant.7.clone.hy_hbm, bf16[2,512,512]{2,1,0:T(8,128)(2,1)} %constant.8.clone.wz_hbm, f32[4,4]{1,0:T(4,128)} %coup_hbm.1, f32[1,256]{1,0:T(1,128)} %bitcast.5, ...), custom_call_target="tpu_custom_call" | custom-call | tf_op jit(solution)/shard_map/pallas_call | solution.py:257
  57.4 1.3 %copy.10 = f32[4,32,32,128]{3,2,1,0:T(8,128)} copy(f32[4,32,32,128]{3,2,1,0:T(8,128)S(1)} %shard_map.82) | data formatting | bytes 4194304

commit v2 on v1

--- a/solution.py
+++ b/solution.py
@@ -9,9 +9,12 @@
 from jax.sharding import PartitionSpec as P
 
 MESH = pl.DeviceIdType.MESH
+INNER = 6
+OUTER = 18
+PARTS = (4, 4, 4, 4, 4, 4, 4, 2, 2)
+GROUPS = (2, 2, 4)
 WINDOW = 12
-PARTS = (6, 6, 6, 6, 4, 4)
-GROUPS = 4
+LAG = 2
 
 
 def chunk_sizes(block):
@@ -43,7 +46,7 @@
     x_hbm, hx_hbm, hy_hbm, wz_hbm, coup_hbm, sx_hbm, sy_hbm, sz_hbm,
     out_ref,
     x_buf, hx, hy, wz, coup_ref, sx_ref, sy_ref, sz_ref, send_a, recv_b, send_c, recv_d, z_buf, sy_cols,
-    sem_x, sem_t, sem_as, sem_br, sem_cs, sem_dr,
+    sem_x, sem_t, sem_as, sem_br, sem_cs, sem_dr, ready,
 ):
     fields, share_y, share_z, size_x = x_hbm.shape
     size_y, size_z = sy_hbm.shape[1], sz_hbm.shape[1]
@@ -53,9 +56,12 @@
     starts = [sum(sizes[:c]) for c in range(len(sizes))]
     left, right = lax.axis_index("left"), lax.axis_index("right")
     ends = [start + size for start, size in zip(starts, sizes)]
-    groups = GROUPS if pairs % GROUPS == 0 else 1
-    group_y = share_y // groups
-    hops_left = sorted(range(1, n_left), key=lambda j: (abs(2 * j - n_left), j))
+    groups = GROUPS if sum(GROUPS) == pairs else (pairs,)
+    half = n_left // 2
+    side, local = left // half, lax.rem(left, half)
+    near, far = side * half, (1 - side) * half
+    across = [far + side * k + (1 - side) * (half - 1 - k) for k in range(half)]
+    beside = [near + lax.rem(local + k, half) for k in range(1, half)]
     hops_right = sorted(range(1, n_right), key=lambda j: (abs(2 * j - n_right), j))
 
     table_copies = [
@@ -72,10 +78,14 @@
         )
 
     barrier = pltpu.get_barrier_semaphore()
-    for j in hops_left:
-        pl.semaphore_signal(
-            barrier, inc=1, device_id=(lax.rem(left + j, n_left), right), device_id_type=MESH
-        )
+    for other in across:
+        pl.semaphore_signal(barrier, inc=1, device_id=(other, right), device_id_type=MESH)
+    for k in range(1, half):
+        @pl.when(local < k)
+        def _():
+            pl.semaphore_signal(
+                barrier, inc=1, device_id=(near + k, right), device_id_type=MESH
+            )
     for j in hops_right:
         pl.semaphore_signal(
             barrier, inc=1, device_id=(left, lax.rem(right + j, n_right)), device_id_type=MESH
@@ -86,16 +96,13 @@
     for copy in table_copies[1:]:
         copy.start()
 
-    def left_copy(chunk, j, first_y=0, count_y=share_y):
-        other = lax.rem(left + j, n_left)
+    def left_copy(chunk, other, first_y=0, count_y=share_y):
         start, size = starts[chunk], sizes[chunk]
         return pltpu.make_async_remote_copy(
             src_ref=send_a.at[
                 pl.ds(start * n_left + other * size, size), pl.ds(first_y, count_y)
             ],
-            dst_ref=recv_b.at[
-                pl.ds(start, size), pl.ds(left * share_y + first_y, count_y)
-            ],
+            dst_ref=recv_b.at[left, pl.ds(start, size), pl.ds(first_y, count_y)],
             send_sem=sem_as.at[0],
             recv_sem=sem_br.at[chunk],
             device_id=(other, right),
@@ -119,7 +126,7 @@
 
     def left_arrived(chunk):
         rows = pl.ds(starts[chunk], sizes[chunk])
-        wait_bytes(recv_b.at[rows, pl.ds(0, (n_left - 1) * share_y)], sem_br.at[chunk])
+        wait_bytes(recv_b.at[pl.ds(0, n_left - 1), rows], sem_br.at[chunk])
 
     def right_arrived(chunk):
         rows = pl.ds(starts[chunk], sizes[chunk])
@@ -145,37 +152,50 @@
         return carry
 
     table_copies[0].wait()
-    per_group = pairs // groups
-    for group in range(groups):
-        lax.fori_loop(group * per_group, (group + 1) * per_group, x_step, 0)
-        if group == 0:
-            pl.semaphore_wait(barrier, n_left + n_right - 2)
-        for j in hops_left:
-            left_copy(0, j, group * group_y, group_y).start()
-
-    def left_start(after, upto):
+    done = 0
+    for count in groups:
+        lax.fori_loop(done, done + count, x_step, 0)
+        if done == 0:
+            pl.semaphore_wait(barrier, half + local + n_right - 1)
+        for other in across:
+            left_copy(0, other, 2 * done, 2 * count).start()
+        if done == 0:
+            for k in range(half - 1):
+                @pl.when(k < local)
+                def _():
+                    pl.semaphore_signal(
+                        ready, inc=1, device_id=(near + k, right), device_id_type=MESH
+                    )
+        done += count
+
+    @pl.when(local < half - 1)
+    def _():
+        pl.semaphore_wait(ready, half - 1 - local)
+
+    for other in beside:
+        left_copy(0, other).start()
+
+    def left_advance(before, now):
         for chunk in range(1, len(sizes)):
-            if after < ends[chunk] <= upto:
-                for j in hops_left:
-                    left_copy(chunk, j).start()
-
-    left_start(ends[0], max(WINDOW, ends[0]))
+            if before + WINDOW < ends[chunk] <= now + WINDOW:
+                for other in across + beside:
+                    left_copy(chunk, other).start()
+
+    left_advance(-block_x, 0)
 
     for start, size in zip(starts, sizes):
-        recv_b[pl.ds(start, size), pl.ds(left * share_y, share_y)] = send_a[
-            pl.ds(start * n_left + left * size, size)
-        ]
+        recv_b[left, pl.ds(start, size)] = send_a[pl.ds(start * n_left + left * size, size)]
     for copy in table_copies[1:]:
         copy.wait()
     sy_cols[...] = jnp.broadcast_to(sy_ref[...], (size_z, size_y)).T
 
     def y_stage(chunk):
         left_arrived(chunk)
-        left_start(max(starts[chunk] + WINDOW, ends[0]), ends[chunk] + WINDOW)
+        left_advance(starts[chunk], ends[chunk])
         start, size = starts[chunk], sizes[chunk]
 
         def y_step(step, carry):
-            rows = [recv_b[start + 2 * step + i] for i in range(2)]
+            rows = [recv_b[:, start + 2 * step + i].reshape(size_y, lanes) for i in range(2)]
             high, low = split(jnp.concatenate(rows, axis=1))
             dot = functools.partial(jnp.dot, preferred_element_type=jnp.float32)
             both = dot(hy[...], high)
@@ -200,7 +220,8 @@
         ]
         high, low = split(jnp.concatenate(lines, axis=1))
         dot = functools.partial(jnp.dot, preferred_element_type=jnp.float32)
-        z_buf[:count] = dot(high, wz[0]) + dot(low, wz[0]) + dot(high, wz[1])
+        both = dot(jnp.concatenate([high, low], axis=0), wz[0])
+        z_buf[:count] = both[:count] + both[count:] + dot(high, wz[1])
 
         part_y = sy_cols[pl.ds(pl.multiple_of(right * block_y, block_y), block_y), :]
 
@@ -221,9 +242,10 @@
 
     for chunk in range(len(sizes)):
         y_stage(chunk)
-        if chunk:
-            z_stage(chunk - 1)
-    z_stage(len(sizes) - 1)
+        if chunk >= LAG:
+            z_stage(chunk - LAG)
+    for chunk in range(max(len(sizes) - LAG, 0), len(sizes)):
+        z_stage(chunk)
 
     wait_bytes(send_a.at[pl.ds(0, (n_left - 1) * block_x)], sem_as.at[0])
     wait_bytes(send_c.at[pl.ds(0, n_right - 1)], sem_cs.at[0])
@@ -269,7 +291,7 @@
                 pltpu.VMEM((1, size_y), f32),
                 pltpu.VMEM((1, size_z), f32),
                 pltpu.VMEM((size_x, share_y, lanes), f32),
-                pltpu.VMEM((block_x, size_y, lanes), f32),
+                pltpu.VMEM((n_left, block_x, share_y, lanes), f32),
                 pltpu.VMEM((n_right, block_x, block_y, lanes), f32),
                 pltpu.VMEM((n_right, block_x, block_y, lanes), f32),
                 pltpu.VMEM((max(sizes) * block_y, fields * size_z), f32),
@@ -280,6 +302,7 @@
                 pltpu.SemaphoreType.DMA((chunks,)),
                 pltpu.SemaphoreType.DMA((1,)),
                 pltpu.SemaphoreType.DMA((chunks,)),
+                pltpu.SemaphoreType.REGULAR,
             ],
             compiler_params=pltpu.CompilerParams(
                 collective_id=0, has_side_effects=True, vmem_limit_bytes=room

time: 58.9 us -> 58 us (0.985)
  Pallas kernels: 57.4 us -> 56.5 us
    pallas_call x1, Pallas kernels: 57.4 us -> 56.5 us  [body(): pl.pallas_call(functools.partial(kernel, n_left, n_right, sizes), out_sha...]
where the time goes in v2:
time: 58 us; the launch traced here: 57.8 us
  Pallas kernels  56.5 us (97%)
  local copies, waits for them, and re-layouts  1.32 us (2%)
    pallas_call x1, Pallas kernels, body(): pl.pallas_call(functools.partial(kernel, n_left, n_right, sizes), out_sha...  56.5 us
    unnamed x1, local copies, waits for them, and re-layouts  1.32 us

profile of v2, /device:TPU:0, one launch (start us, length us, event | category | flops | bytes accessed | tf_op | source)
XLA Modules:
  0.0 57.8 jit_solution(6615047815051200319)
XLA Ops:
  0.0 56.5 %shard_map.82 = f32[4,32,32,128]{3,2,1,0:T(8,128)S(1)} custom-call(f32[4,16,32,256]{3,2,1,0:T(8,128)} %bitcast.4, bf16[512,256]{1,0:T(8,128)(2,1)} %constant.6.clone.hx_hbm, bf16[256,128]{1,0:T(8,128)(2,1)} %constant.7.clone.hy_hbm, bf16[2,512,512]{2,1,0:T(8,128)(2,1)} %constant.8.clone.wz_hbm, f32[4,4]{1,0:T(4,128)} %coup_hbm.1, f32[1,256]{1,0:T(1,128)} %bitcast.5, ...), custom_call_target="tpu_custom_call" | custom-call | tf_op jit(solution)/shard_map/pallas_call | solution.py:279
  56.5 1.3 %copy.10 = f32[4,32,32,128]{3,2,1,0:T(8,128)} copy(f32[4,32,32,128]{3,2,1,0:T(8,128)S(1)} %shard_map.82) | data formatting | bytes 4194304

commit v3 on v2

--- a/solution.py
+++ b/solution.py
@@ -14,6 +14,9 @@
 PARTS = (4, 4, 4, 4, 4, 4, 4, 2, 2)
 GROUPS = (2, 2, 4)
 WINDOW = 12
+TAIL = 2
+BACK = 8
+WIDE = 2
 LAG = 2
 
 
@@ -134,9 +137,13 @@
 
     flat_a = send_a.reshape(size_x * share_y, lanes)
 
-    def x_step(pair, carry):
-        x_copy(pair).wait()
-        planes = [x_buf[pair, :, i].reshape(lanes, size_x) for i in range(2)]
+    wide = WIDE if all(count % WIDE == 0 for count in groups) else 1
+
+    def x_step(step, carry):
+        planes = []
+        for i in range(wide):
+            x_copy(step * wide + i).wait()
+            planes += [x_buf[step * wide + i, :, k].reshape(lanes, size_x) for k in range(2)]
         high, low = split(jnp.concatenate(planes, axis=0))
         dot = functools.partial(
             lax.dot_general,
@@ -145,8 +152,8 @@
         )
         both = dot(hx[...], high)
         modes = both[:size_x] + both[size_x:] + dot(hx[:size_x], low)
-        for i in range(2):
-            flat_a[pl.ds(2 * pair + i, size_x, stride=share_y), :] = modes[
+        for i in range(2 * wide):
+            flat_a[pl.ds(2 * wide * step + i, size_x, stride=share_y), :] = modes[
                 :, i * lanes:(i + 1) * lanes
             ]
         return carry
@@ -154,7 +161,7 @@
     table_copies[0].wait()
     done = 0
     for count in groups:
-        lax.fori_loop(done, done + count, x_step, 0)
+        lax.fori_loop(done // wide, (done + count) // wide, x_step, 0)
         if done == 0:
             pl.semaphore_wait(barrier, half + local + n_right - 1)
         for other in across:
@@ -178,7 +185,10 @@
     def left_advance(before, now):
         for chunk in range(1, len(sizes)):
             if before + WINDOW < ends[chunk] <= now + WINDOW:
-                for other in across + beside:
+                left_copy(chunk, across[0]).start()
+            window = WINDOW if chunk < len(sizes) - TAIL else BACK
+            if before + window < ends[chunk] <= now + window:
+                for other in across[1:] + beside:
                     left_copy(chunk, other).start()
 
     left_advance(-block_x, 0)

time: 58 us -> 56.9 us (0.981)
  Pallas kernels: 56.5 us -> 55.5 us
    pallas_call x1, Pallas kernels: 56.5 us -> 55.5 us  [body(): pl.pallas_call(functools.partial(kernel, n_left, n_right, sizes), out_sha...]
where the time goes in v3:
time: 56.9 us; the launch traced here: 56.8 us
  Pallas kernels  55.5 us (98%)
  local copies, waits for them, and re-layouts  1.32 us (2%)
    pallas_call x1, Pallas kernels, body(): pl.pallas_call(functools.partial(kernel, n_left, n_right, sizes), out_sha...  55.5 us
    unnamed x1, local copies, waits for them, and re-layouts  1.32 us

profile of v3, /device:TPU:0, one launch (start us, length us, event | category | flops | bytes accessed | tf_op | source)
XLA Modules:
  0.0 56.8 jit_solution(1518256897570573730)
XLA Ops:
  0.0 55.5 %shard_map.82 = f32[4,32,32,128]{3,2,1,0:T(8,128)S(1)} custom-call(f32[4,16,32,256]{3,2,1,0:T(8,128)} %bitcast.4, bf16[512,256]{1,0:T(8,128)(2,1)} %constant.6.clone.hx_hbm, bf16[256,128]{1,0:T(8,128)(2,1)} %constant.7.clone.hy_hbm, bf16[2,512,512]{2,1,0:T(8,128)(2,1)} %constant.8.clone.wz_hbm, f32[4,4]{1,0:T(4,128)} %coup_hbm.1, f32[1,256]{1,0:T(1,128)} %bitcast.5, ...), custom_call_target="tpu_custom_call" | custom-call | tf_op jit(solution)/shard_map/pallas_call | solution.py:289
  55.5 1.3 %copy.10 = f32[4,32,32,128]{3,2,1,0:T(8,128)} copy(f32[4,32,32,128]{3,2,1,0:T(8,128)S(1)} %shard_map.82) | data formatting | bytes 4194304

commit v4 on v3

--- a/solution.py
+++ b/solution.py
@@ -17,7 +17,9 @@
 TAIL = 2
 BACK = 8
 WIDE = 2
+TALL = 4
 LAG = 2
+HOLD = 3
 
 
 def chunk_sizes(block):
@@ -186,7 +188,7 @@
         for chunk in range(1, len(sizes)):
             if before + WINDOW < ends[chunk] <= now + WINDOW:
                 left_copy(chunk, across[0]).start()
-            window = WINDOW if chunk < len(sizes) - TAIL else BACK
+            window = BACK if chunk >= len(sizes) - TAIL else WINDOW
             if before + window < ends[chunk] <= now + window:
                 for other in across[1:] + beside:
                     left_copy(chunk, other).start()
@@ -204,19 +206,22 @@
         left_advance(starts[chunk], ends[chunk])
         start, size = starts[chunk], sizes[chunk]
 
+        tall = TALL if size % TALL == 0 else 2
+
         def y_step(step, carry):
-            rows = [recv_b[:, start + 2 * step + i].reshape(size_y, lanes) for i in range(2)]
+            first = start + tall * step
+            rows = [recv_b[:, first + i].reshape(size_y, lanes) for i in range(tall)]
             high, low = split(jnp.concatenate(rows, axis=1))
             dot = functools.partial(jnp.dot, preferred_element_type=jnp.float32)
             both = dot(hy[...], high)
             modes = both[:size_y] + both[size_y:] + dot(hy[:size_y], low)
-            for i in range(2):
-                send_c[:, start + 2 * step + i] = modes[:, i * lanes:(i + 1) * lanes].reshape(
+            for i in range(tall):
+                send_c[:, first + i] = modes[:, i * lanes:(i + 1) * lanes].reshape(
                     n_right, block_y, lanes
                 )
             return carry
 
-        lax.fori_loop(0, size // 2, y_step, 0)
+        lax.fori_loop(0, size // tall, y_step, 0)
         for j in hops_right:
             right_copy(chunk, j).start()
         recv_d[right, pl.ds(start, size)] = send_c[right, pl.ds(start, size)]
@@ -252,9 +257,9 @@
 
     for chunk in range(len(sizes)):
         y_stage(chunk)
-        if chunk >= LAG:
+        if LAG <= chunk < len(sizes) - HOLD:
             z_stage(chunk - LAG)
-    for chunk in range(max(len(sizes) - LAG, 0), len(sizes)):
+    for chunk in range(max(len(sizes) - HOLD - LAG, 0), len(sizes)):
         z_stage(chunk)
 
     wait_bytes(send_a.at[pl.ds(0, (n_left - 1) * block_x)], sem_as.at[0])

time: 56.9 us -> 56.9 us (level)
  no operation moved by 1% of the time
where the time goes in v4:
time: 56.9 us; the launch traced here: 56.7 us
  Pallas kernels  55.4 us (97%)
  local copies, waits for them, and re-layouts  1.32 us (2%)
    pallas_call x1, Pallas kernels, body(): pl.pallas_call(functools.partial(kernel, n_left, n_right, sizes), out_sha...  55.4 us
    unnamed x1, local copies, waits for them, and re-layouts  1.32 us

profile of v4, /device:TPU:0, one launch (start us, length us, event | category | flops | bytes accessed | tf_op | source)
XLA Modules:
  0.0 56.7 jit_solution(16681586589633417505)
XLA Ops:
  0.0 55.4 %shard_map.82 = f32[4,32,32,128]{3,2,1,0:T(8,128)S(1)} custom-call(f32[4,16,32,256]{3,2,1,0:T(8,128)} %bitcast.4, bf16[512,256]{1,0:T(8,128)(2,1)} %constant.6.clone.hx_hbm, bf16[256,128]{1,0:T(8,128)(2,1)} %constant.7.clone.hy_hbm, bf16[2,512,512]{2,1,0:T(8,128)(2,1)} %constant.8.clone.wz_hbm, f32[4,4]{1,0:T(4,128)} %coup_hbm.1, f32[1,256]{1,0:T(1,128)} %bitcast.5, ...), custom_call_target="tpu_custom_call" | custom-call | tf_op jit(solution)/shard_map/pallas_call | solution.py:294
  55.4 1.3 %copy.10 = f32[4,32,32,128]{3,2,1,0:T(8,128)} copy(f32[4,32,32,128]{3,2,1,0:T(8,128)S(1)} %shard_map.82) | data formatting | bytes 4194304

commit v5 on v4

--- a/solution.py
+++ b/solution.py
@@ -9,13 +9,11 @@
 from jax.sharding import PartitionSpec as P
 
 MESH = pl.DeviceIdType.MESH
-INNER = 6
-OUTER = 18
-PARTS = (4, 4, 4, 4, 4, 4, 4, 2, 2)
+PARTS = (4, 4, 4, 4, 4, 4, 2, 2, 2, 2)
 GROUPS = (2, 2, 4)
 WINDOW = 12
 TAIL = 2
-BACK = 8
+BACK = 6
 WIDE = 2
 TALL = 4
 LAG = 2

time: 56.9 us -> 56.4 us (level)
  no operation moved by 1% of the time
where the time goes in v5:
time: 56.4 us; the launch traced here: 56.2 us
  Pallas kernels  54.9 us (97%)
  local copies, waits for them, and re-layouts  1.32 us (2%)
    pallas_call x1, Pallas kernels, body(): pl.pallas_call(functools.partial(kernel, n_left, n_right, sizes), out_sha...  54.9 us
    unnamed x1, local copies, waits for them, and re-layouts  1.32 us

profile of v5, /device:TPU:0, one launch (start us, length us, event | category | flops | bytes accessed | tf_op | source)
XLA Modules:
  0.0 56.2 jit_solution(11174180110286397075)
XLA Ops:
  0.0 54.9 %shard_map.82 = f32[4,32,32,128]{3,2,1,0:T(8,128)S(1)} custom-call(f32[4,16,32,256]{3,2,1,0:T(8,128)} %bitcast.4, bf16[512,256]{1,0:T(8,128)(2,1)} %constant.6.clone.hx_hbm, bf16[256,128]{1,0:T(8,128)(2,1)} %constant.7.clone.hy_hbm, bf16[2,512,512]{2,1,0:T(8,128)(2,1)} %constant.8.clone.wz_hbm, f32[4,4]{1,0:T(4,128)} %coup_hbm.1, f32[1,256]{1,0:T(1,128)} %bitcast.5, ...), custom_call_target="tpu_custom_call" | custom-call | tf_op jit(solution)/shard_map/pallas_call | solution.py:292
  54.9 1.3 %copy.10 = f32[4,32,32,128]{3,2,1,0:T(8,128)} copy(f32[4,32,32,128]{3,2,1,0:T(8,128)S(1)} %shard_map.82) | data formatting | bytes 4194304

commit v6 on v5

--- a/solution.py
+++ b/solution.py
@@ -13,7 +13,7 @@
 GROUPS = (2, 2, 4)
 WINDOW = 12
 TAIL = 2
-BACK = 6
+BACK = 4
 WIDE = 2
 TALL = 4
 LAG = 2

time: 56.4 us -> 56.4 us (level)
  no operation moved by 1% of the time
where the time goes in v6:
time: 56.4 us; the launch traced here: 56 us
  Pallas kernels  54.7 us (97%)
  local copies, waits for them, and re-layouts  1.32 us (2%)
    pallas_call x1, Pallas kernels, body(): pl.pallas_call(functools.partial(kernel, n_left, n_right, sizes), out_sha...  54.7 us
    unnamed x1, local copies, waits for them, and re-layouts  1.32 us

profile of v6, /device:TPU:0, one launch (start us, length us, event | category | flops | bytes accessed | tf_op | source)
XLA Modules:
  0.0 56.0 jit_solution(15791987128842717610)
XLA Ops:
  0.0 54.7 %shard_map.82 = f32[4,32,32,128]{3,2,1,0:T(8,128)S(1)} custom-call(f32[4,16,32,256]{3,2,1,0:T(8,128)} %bitcast.4, bf16[512,256]{1,0:T(8,128)(2,1)} %constant.6.clone.hx_hbm, bf16[256,128]{1,0:T(8,128)(2,1)} %constant.7.clone.hy_hbm, bf16[2,512,512]{2,1,0:T(8,128)(2,1)} %constant.8.clone.wz_hbm, f32[4,4]{1,0:T(4,128)} %coup_hbm.1, f32[1,256]{1,0:T(1,128)} %bitcast.5, ...), custom_call_target="tpu_custom_call" | custom-call | tf_op jit(solution)/shard_map/pallas_call | solution.py:292
  54.7 1.3 %copy.10 = f32[4,32,32,128]{3,2,1,0:T(8,128)} copy(f32[4,32,32,128]{3,2,1,0:T(8,128)S(1)} %shard_map.82) | data formatting | bytes 4194304
